TPU v7x, 8 devices: a whole 2x2x1 slice. The times are simulated.
8 devices in a mesh: stage: 4 (over z, y, x), expert: 2 (over core).
Axes of the slice: x: 2, y: 2, z: 1, core: 2. Of those that a mesh axis runs over, the one named last changes fastest.
Arguments:
- w_gate: bfloat16 [8, 16, 1024, 512], P('stage', 'expert')
- w_up: bfloat16 [8, 16, 1024, 512], P('stage', 'expert')
- w_down: bfloat16 [8, 16, 512, 1024], P('stage', 'expert')
- hot_units: int32 [2], replicated
- slot_map: int32 [8, 2], replicated
Outputs:
- output 1: bfloat16 [8, 32, 1024, 1024], P(None, ('stage', 'expert'))
- output 2: bfloat16 [8, 32, 512, 1024], P(None, ('stage', 'expert'))
All inputs are finite; a program needn't handle non-finite values.
Results may differ from a plain program's by a relative error of at most 0.001.
Values are sent between devices in bfloat16 or wider.
A program may use at most 1 GiB of HBM per device.

v0:
```python
import jax
import jax.numpy as jnp
from jax import lax
from jax.sharding import PartitionSpec as P


def solution(mesh):
    stage_count = mesh.shape['stage']
    group_count = mesh.shape['expert']
    devices_flat = stage_count * group_count
    flat_axes = ('stage', 'expert')
    perm_pairs = [(stage_idx * group_count + rank_idx, rank_idx * stage_count + stage_idx) for stage_idx in range(stage_count) for rank_idx in range(group_count)]

    def local_handover(gate_blk, up_blk, down_blk, hot_units, slot_map):
        layers_stage, experts_rank, d_model, ff_expert = gate_blk.shape
        layers = layers_stage * stage_count
        experts = experts_rank * group_count
        split_count = max(devices_flat // experts, 1)
        units_dev = max(experts // devices_flat, 1)
        ff_dev = ff_expert // split_count
        gate_parts = gate_blk.reshape(layers_stage, experts_rank, d_model, split_count, ff_dev)
        up_parts = up_blk.reshape(layers_stage, experts_rank, d_model, split_count, ff_dev)
        fused_send = jnp.concatenate([gate_parts, up_parts], axis=-1).transpose(0, 1, 3, 2, 4).reshape(layers_stage, stage_count, units_dev, d_model, 2 * ff_dev)
        down_send = down_blk.reshape(layers_stage, stage_count, units_dev, ff_dev, d_model)
        fused_recv = lax.all_to_all(fused_send, 'stage', 1, 0, tiled=True).reshape(layers, units_dev, d_model, 2 * ff_dev)
        down_recv = lax.all_to_all(down_send, 'stage', 1, 0, tiled=True).reshape(layers, units_dev, ff_dev, d_model)
        fused_home = lax.ppermute(fused_recv, flat_axes, perm_pairs)
        down_home = lax.ppermute(down_recv, flat_axes, perm_pairs)
        my_flat = lax.axis_index('stage') * group_count + lax.axis_index('expert')
        owned_mask = (hot_units // units_dev == my_flat)[None, :, None, None]
        local_pick = hot_units % units_dev
        fused_hot = lax.psum(jnp.where(owned_mask, jnp.take(fused_home, local_pick, axis=1), 0), flat_axes)
        down_hot = lax.psum(jnp.where(owned_mask, jnp.take(down_home, local_pick, axis=1), 0), flat_axes)
        my_slots = lax.dynamic_index_in_dim(slot_map, my_flat, axis=0, keepdims=False)
        slot_used = (my_slots >= 0)[None, :, None, None]
        hot_pick = jnp.maximum(my_slots, 0)
        fused_extra = jnp.where(slot_used, jnp.take(fused_hot, hot_pick, axis=1), 0)
        down_extra = jnp.where(slot_used, jnp.take(down_hot, hot_pick, axis=1), 0)
        return jnp.concatenate([fused_home, fused_extra], axis=1), jnp.concatenate([down_home, down_extra], axis=1)

    return jax.shard_map(local_handover, mesh=mesh, in_specs=(P('stage', 'expert'), P('stage', 'expert'), P('stage', 'expert'), P(), P()), out_specs=(P(None, flat_axes), P(None, flat_axes)), check_vma=False)
```

profile of v0, /device:TPU:0, one launch (start us, length us, event | category | flops | bytes accessed | tf_op | source)
XLA Modules:
  0.0 2810.8 jit_solution(5107521012115676561)
XLA Ops:
  7.2 22.7 pad_maximum_fusion.1
  29.9 23.0 copy.34
  52.9 9.7 all-to-all-start
  62.6 13.9 copy.25
  76.6 350.3 %all-to-all-done = bf16[2,4,2,1024,1024]{4,3,2,0,1:T(8,128)(2,1)} async-done(((bf16[2,4,2,1024,1024]{4,3,2,0,1:T(8,128)(2,1)}), bf16[2,4,2,1024,1024]{4,3,2,0,1:T(8,128)(2,1)}, u32[]{:S(2)}, u32[]{:S(2)}) %all-to-all-start) | async-done | bytes 33554464 | tf_op jit(solution)/shard_map/all_to_all | solution.py:25
  426.8 7.0 all-to-all-start.1
  433.9 252.0 %collective-permute-start = (bf16[8,2,1024,1024]{3,2,1,0:T(8,128)(2,1)}, bf16[8,2,1024,1024]{3,2,1,0:T(8,128)(2,1)}, u32[]{:S(2)}, u32[]{:S(2)}) collective-permute-start(bf16[8,2,1024,1024]{3,2,1,0:T(8,128)(2,1)} %bitcast.4), channel_id=1, source_target_pairs={{0,0},{1,4},{2,1},{3,5},{4,2},{5,6},{6,3},{7,7}} | collective-permute-start | bytes 100663304 | tf_op jit(solution)/shard_map/ppermute | solution.py:27
  685.9 126.8 %collective-permute-start.1 = (bf16[8,2,512,1024]{3,2,1,0:T(8,128)(2,1)}, bf16[8,2,512,1024]{3,2,1,0:T(8,128)(2,1)}, u32[]{:S(2)}, u32[]{:S(2)}) collective-permute-start(bf16[8,2,512,1024]{3,2,1,0:T(8,128)(2,1)} %bitcast.26), channel_id=1, source_target_pairs={{0,0},{1,4},{2,1},{3,5},{4,2},{5,6},{6,3},{7,7}} | collective-permute-start | bytes 50331656 | tf_op jit(solution)/shard_map/ppermute | solution.py:28
  812.8 12.4 fusion.7
  827.6 8.7 while.64
  838.7 8.6 while.65
  849.7 8.6 while.66
  860.8 8.6 while.67
  869.3 15.3 fusion
  884.6 22.8 fusion.5
  909.9 8.8 while.48
  918.7 4.8 bitcast_dynamic-update-slice_fusion.39
  926.0 8.8 while.49
  937.3 8.8 while.50
  948.6 8.8 while.51
  960.0 8.9 while.52
  965.1 3.8 bitcast_dynamic-update-slice_fusion.68
  971.4 8.8 while.53
  982.7 8.8 while.54
  994.1 8.8 while.55
  1002.9 5.0 bitcast_dynamic-update-slice_fusion.38
  1028.8 22.8 select_select_fusion.1
  1052.7 1447.8 %all-reduce.3.cloned.1.call-done = (bf16[8,2,1024,1024]{3,2,1,0:T(8,128)(2,1)}, bf16[8,2,512,1024]{3,2,1,0:T(8,128)(2,1)}) async-done(((bf16[8,2,1024,1024]{3,2,1,0:T(8,128)(2,1)}, bf16[8,2,512,1024]{3,2,1,0:T(8,128)(2,1)}), (bf16[8,2,1024,1024]{3,2,1,0:T(8,128)(2,1)}, bf16[8,2,512,1024]{3,2,1,0:T(8,128)(2,1)})) %all-reduce.3.cloned.1.call-update) | async-done | bytes 50331664 | tf_op jit(solution)/shard_map/psum | solution.py:32
  2500.5 12.4 fusion.6
  2515.2 8.4 while.68
  2526.0 8.5 while.69
  2536.8 8.5 while.70
  2547.8 8.6 while.71
  2556.4 22.8 fusion.4
  2581.8 8.6 while.56
  2590.4 4.8 bitcast_dynamic-update-slice_fusion.31
  2597.8 8.5 while.57
  2608.9 8.5 while.58
  2619.8 8.4 while.59
  2630.8 8.5 while.60
  2641.8 8.5 while.61
  2652.8 8.5 while.62
  2663.8 8.5 while.63
  2672.3 5.0 bitcast_dynamic-update-slice_fusion.30
  2698.2 22.8 select_select_fusion
  2721.0 15.3 fusion.1
  2736.3 22.9 pad_maximum_fusion.2
  2759.2 44.7 %pad_maximum_fusion = bf16[8,4,1024,1024]{3,2,1,0:T(8,128)(2,1)} fusion(bf16[8,2,1024,1024]{3,2,1,0:T(8,128)(2,1)} %select_select_fusion, bf16[8,2,1024,1024]{3,2,1,0:T(8,128)(2,1)} %collective-permute-done), kind=kLoop, calls=%fused_computation.48 | loop fusion | flops 33554432 | bytes 134217728 | tf_op jit(solution)/shard_map/concatenate | solution.py:39
  (169 shorter events, 305.9 us)
Async XLA Ops:
  52.9 374.0 %all-to-all-start = ((bf16[2,4,2,1024,1024]{4,3,2,0,1:T(8,128)(2,1)}), bf16[2,4,2,1024,1024]{4,3,2,0,1:T(8,128)(2,1)}, u32[]{:S(2)}, u32[]{:S(2)}) async-start(bf16[2,4,2,1024,1024]{4,3,2,0,1:T(8,128)(2,1)} %copy.34), calls=%async_computation | async-start | bytes 67108864 | tf_op jit(solution)/shard_map/all_to_all | solution.py:25
  76.6 736.2 %copy-start.13 = (s32[2]{0:T(128)S(1)}, s32[2]{0:T(128)}, u32[]{:S(2)}) copy-start(s32[2]{0:T(128)} %param.12) | copy-start | bytes 28
  426.8 259.0 %all-to-all-start.1 = ((bf16[2,4,2,512,1024]{4,3,2,0,1:T(8,128)(2,1)}), bf16[2,4,2,512,1024]{4,3,2,0,1:T(8,128)(2,1)}, u32[]{:S(2)}, u32[]{:S(2)}) async-start(bf16[2,4,2,512,1024]{4,3,2,0,1:T(8,128)(2,1)} %copy.25), calls=%async_computation.1 | async-start | bytes 33554432 | tf_op jit(solution)/shard_map/all_to_all | solution.py:26
  433.9 2066.6 %all-reduce.3.cloned.1.call-start = ((), (), s32[]{:S(2)}) async-start(), calls=%async_computation.2 | async-start | bytes 100663296 | tf_op jit(solution)/shard_map/psum | solution.py:32
  433.9 450.7 %collective-permute-start = (bf16[8,2,1024,1024]{3,2,1,0:T(8,128)(2,1)}, bf16[8,2,1024,1024]{3,2,1,0:T(8,128)(2,1)}, u32[]{:S(2)}, u32[]{:S(2)}) collective-permute-start(bf16[8,2,1024,1024]{3,2,1,0:T(8,128)(2,1)} %bitcast.4), channel_id=1, source_target_pairs={{0,0},{1,4},{2,1},{3,5},{4,2},{5,6},{6,3},{7,7}} | collective-permute-start | bytes 100663304 | tf_op jit(solution)/shard_map/ppermute | solution.py:27
  685.9 126.9 %collective-permute-start.1 = (bf16[8,2,512,1024]{3,2,1,0:T(8,128)(2,1)}, bf16[8,2,512,1024]{3,2,1,0:T(8,128)(2,1)}, u32[]{:S(2)}, u32[]{:S(2)}) collective-permute-start(bf16[8,2,512,1024]{3,2,1,0:T(8,128)(2,1)} %bitcast.26), channel_id=1, source_target_pairs={{0,0},{1,4},{2,1},{3,5},{4,2},{5,6},{6,3},{7,7}} | collective-permute-start | bytes 50331656 | tf_op jit(solution)/shard_map/ppermute | solution.py:28
  1002.9 5.0 copy-start.1
  1007.8 3.7 copy-start.2
  1011.5 3.7 copy-start.3
  1015.2 3.7 copy-start.4
  1018.9 3.7 copy-start.5
  1022.6 3.7 copy-start.6
  1051.6 0.7 copy-start.12
  2672.3 5.0 copy-start.7
  2677.2 3.7 copy-start.8
  2681.0 3.7 copy-start.9
  2684.7 3.7 copy-start.10
  2688.4 3.7 copy-start.11
  2692.1 3.7 copy-start
Sparse Core Ops, SparseCore 0:
  1051.7 1448.6 all-reduce.2
where the time goes:
time: 2840 us; the launch traced here: 2810 us
  waiting for transfers between devices  1800 us (63%)
  local copies, waits for them, and re-layouts  436 us (15%)
  starting transfers between devices  396 us (14%)
  other arithmetic  167 us (6%)
    psum x1, waiting for transfers between devices, local_handover(): lax.psum(jnp.where(owned_mask, jnp.take(fused_home, local_pick, axis=1),...  1450 us
    all_to_all x1, waiting for transfers between devices, local_handover(): lax.all_to_all(fused_send, 'stage', 1, 0, tiled=True)  350 us
    ppermute x1, starting transfers between devices, local_handover(): fused_home = lax.ppermute(fused_recv, flat_axes, perm_pairs)  252 us
    ppermute x1, starting transfers between devices, local_handover(): down_home = lax.ppermute(down_recv, flat_axes, perm_pairs)  127 us
    another operation x49, local copies, waits for them, and re-layouts, local_handover(): jnp.take(fused_home, local_pick, axis=1)  114 us
    another operation x33, local copies, waits for them, and re-layouts, local_handover(): fused_extra = jnp.where(slot_used, jnp.take(fused_hot, hot_pick, axis=1), 0)  70.4 us
    unnamed x42, local copies, waits for them, and re-layouts  57.2 us
  transfers between devices with their start and end apart: 5, of which 2 were waited for; matrix products, arithmetic and copies ran while one was open for 3% of the time, Pallas kernels for 0%

commit v1 on v0

v1 whole, which is shorter than its diff:
```python
import functools

import jax
import jax.numpy as jnp
from jax import lax
from jax.experimental import pallas as pl
from jax.experimental.pallas import tpu as pltpu
from jax.sharding import PartitionSpec as P

MESH = pl.DeviceIdType.MESH
ANY = pl.BlockSpec(memory_space=pl.ANY)
SMEM = pl.BlockSpec(memory_space=pltpu.SMEM)
BF16 = jnp.bfloat16
LAYERS, LOCAL_LAYERS, LOCAL_EXPERTS, HIDDEN, WIDTH = 8, 2, 8, 1024, 512
SLOTS, HOME, HOT = 4, 2, 2


def coords():
    stage, core = lax.axis_index('stage'), lax.axis_index('expert')
    return stage, core, stage // 2, stage % 2


def pick_kernel(hot_ref, gate, up, down, fused_out, down_out, vf, vd, sem):
    core = lax.axis_index('expert')
    for h in range(HOT):
        unit = hot_ref[h]

        @pl.when(unit // LOCAL_EXPERTS == core)
        def _():
            e = unit % LOCAL_EXPERTS
            ins, outs = [], []
            for a in range(LOCAL_LAYERS):
                ins.append([
                    pltpu.make_async_copy(gate.at[a, e], vf.at[a, :, pl.ds(0, WIDTH)], sem.at[a, 0]),
                    pltpu.make_async_copy(up.at[a, e], vf.at[a, :, pl.ds(WIDTH, WIDTH)], sem.at[a, 1]),
                    pltpu.make_async_copy(down.at[a, e], vd.at[a], sem.at[a, 2])])
                outs.append([
                    pltpu.make_async_copy(vf.at[a], fused_out.at[h, a], sem.at[a, 3]),
                    pltpu.make_async_copy(vd.at[a], down_out.at[h, a], sem.at[a, 4])])
            for group in ins:
                for c in group:
                    c.start()
            for group, out in zip(ins, outs):
                for c in group:
                    c.wait()
                for c in out:
                    c.start()
            for out in outs:
                for c in out:
                    c.wait()


def exchange_kernel(owners, gate, up, down, fused_cand, down_cand, fused_home, down_home, fused_hot, down_hot,
                    send_home, recv_home, send_hot, recv_hot, send_peer, recv_peer):
    stage, core, y, x = coords()
    ops = (gate, up, down)

    def to(xx, yy, cc):
        return (yy * 2 + xx, cc)

    def home_copies(q, cc, near):
        e0 = q * 4 + cc * 2
        rows, units = pl.ds(2 * stage, 2), pl.ds(e0, 2)
        dsts = (fused_home.at[rows, :, :, pl.ds(0, WIDTH)], fused_home.at[rows, :, :, pl.ds(WIDTH, WIDTH)], down_home.at[rows])
        return [pltpu.make_async_remote_copy(
            src_ref=ops[k].at[:, units], dst_ref=dsts[k], send_sem=send_home.at[near, cc, k],
            recv_sem=recv_home.at[stage, k], device_id=to(q, core, cc), device_id_type=MESH) for k in range(3)]

    def hot_copies(h, a, origin, slot, device, sslot):
        layer = 2 * origin + a
        own = slot is None
        srcs = (fused_cand.at[h, a], down_cand.at[h, a]) if own else (fused_hot.at[h, layer], down_hot.at[h, layer])
        dsts = (fused_hot.at[h, layer], down_hot.at[h, layer])
        return srcs, dsts, layer

    def remote(srcs, dsts, ss, rs, device):
        return [pltpu.make_async_remote_copy(src_ref=srcs[k], dst_ref=dsts[k], send_sem=ss.at[k], recv_sem=rs.at[k],
                                             device_id=device, device_id_type=MESH) for k in range(2)]

    xn, yn = to(1 - x, y, core), to(x, 1 - y, core)
    x_stage, y_stage, d_stage = y * 2 + (1 - x), (1 - y) * 2 + x, (1 - y) * 2 + (1 - x)

    def hot_own(h, a):
        return (fused_cand.at[h, a], down_cand.at[h, a])

    def hot_at(h, layer):
        return (fused_hot.at[h, layer], down_hot.at[h, layer])

    def start(copies):
        for c in copies:
            c.start()

    own_sends, forwards, peer = {}, {}, {}
    for h in range(HOT):
        for a in range(2):
            dst = hot_at(h, 2 * stage + a)
            own_sends[h, a] = (remote(hot_own(h, a), dst, send_hot.at[h, a, 0], recv_hot.at[h, a, 0], xn),
                               remote(hot_own(h, a), dst, send_hot.at[h, a, 1], recv_hot.at[h, a, 1], yn))
            via = x_stage if a == 0 else y_stage
            piece = hot_at(h, 2 * via + a)
            forwards[h, a] = remote(piece, piece, send_hot.at[h, a, 2], recv_hot.at[h, a, 2], yn if a == 0 else xn)
            for r, origin in enumerate((stage, x_stage, y_stage, d_stage)):
                piece = hot_at(h, 2 * origin + a)
                peer[h, a, r] = remote(hot_own(h, a) if r == 0 else piece, piece, send_peer.at[h, a, r], recv_peer.at[h, a, r],
                                       (stage, 1 - core))

    def arrived(h, a, r):
        origin = (stage, x_stage, y_stage, d_stage)[r]
        piece = hot_at(h, 2 * origin + a)
        return remote(piece, piece, send_hot.at[h, a, r - 1], recv_hot.at[h, a, r - 1], xn)

    for h in range(HOT):
        @pl.when(core == owners[h])
        def _():
            for a in range(2):
                for group in own_sends[h, a]:
                    start(group)
                start(peer[h, a, 0])

    for cc in range(2):
        @pl.when(jnp.logical_or(core != y, core != cc))
        def _():
            start(home_copies(x, cc, 0))
    for cc in range(2):
        start(home_copies(1 - x, cc, 1))

    for h in range(HOT):
        @pl.when(core == owners[h])
        def _():
            for a in range(2):
                for c in arrived(h, a, a + 1):
                    c.wait_recv()
                start(forwards[h, a])
                start(peer[h, a, a + 1])
            for a in range(2):
                for c in arrived(h, a, 2 - a):
                    c.wait_recv()
                start(peer[h, a, 2 - a])
    for h in range(HOT):
        @pl.when(core == owners[h])
        def _():
            for a in range(2):
                for c in arrived(h, a, 3):
                    c.wait_recv()
                start(peer[h, a, 3])

    for h in range(HOT):
        @pl.when(core == owners[h])
        def _():
            for a in range(2):
                for group in (*own_sends[h, a], forwards[h, a]):
                    for c in group:
                        c.wait_send()
                for r in range(4):
                    for c in peer[h, a, r]:
                        c.wait_send()

        @pl.when(core != owners[h])
        def _():
            for a in range(2):
                for r in range(4):
                    for c in peer[h, a, r]:
                        c.wait_recv()
    for near, q in ((0, x), (1, 1 - x)):
        for cc in range(2):
            def waits():
                for c in home_copies(q, cc, near):
                    c.wait_send()
            if near == 0:
                pl.when(jnp.logical_or(core != y, core != cc))(waits)
            else:
                waits()
    for s in range(4):
        @pl.when(jnp.logical_or(s != stage, core != y))
        def _():
            rows = pl.ds(2 * s, 2)
            dsts = (fused_home.at[rows, :, :, pl.ds(0, WIDTH)], fused_home.at[rows, :, :, pl.ds(WIDTH, WIDTH)], down_home.at[rows])
            for k in range(3):
                pltpu.make_async_remote_copy(
                    src_ref=dsts[k], dst_ref=dsts[k], send_sem=send_home.at[0, 0, k], recv_sem=recv_home.at[s, k],
                    device_id=xn, device_id_type=MESH).wait_recv()


DEPTH, LAG = 10, 5


def place_kernel(hot_ref, map_ref, gate, up, down, fused_cand, down_cand, fused_home, down_home, fused_hot, down_hot,
                 fused_out, down_out, vf, vd, zf, zd, in_sem, out_sem, zero_sem):
    stage, core, y, x = coords()
    flat = stage * 2 + core
    zf[...] = jnp.zeros_like(zf)
    zd[...] = jnp.zeros_like(zd)
    items = [(l, t) for t in range(SLOTS) for l in range(LAYERS)]

    def inputs(k):
        l, t = items[k]
        b = k % DEPTH
        bf, bd = vf.at[b], vd.at[b]
        own = stage == l // 2
        if t < HOME:
            whole = lambda f, d: [pltpu.make_async_copy(f, bf, in_sem.at[b, 0]), pltpu.make_async_copy(d, bd, in_sem.at[b, 1])]
            e = x * 4 + core * 2 + t
            a = l % 2
            direct = jnp.logical_and(own, core == y)
            parts = [pltpu.make_async_copy(gate.at[a, e], bf.at[:, pl.ds(0, WIDTH)], in_sem.at[b, 0]),
                     pltpu.make_async_copy(up.at[a, e], bf.at[:, pl.ds(WIDTH, WIDTH)], in_sem.at[b, 2]),
                     pltpu.make_async_copy(down.at[a, e], bd, in_sem.at[b, 1])]
            return [(direct, parts), (jnp.logical_not(direct), whole(fused_home.at[l, t], down_home.at[l, t]))]
        h = map_ref[flat, t - HOME]
        used = h >= 0
        hh = jnp.maximum(h, 0)
        direct = jnp.logical_and(own, hot_ref[hh] // LOCAL_EXPERTS == core)
        copies = lambda f, d: [pltpu.make_async_copy(f, bf, in_sem.at[b, 0]), pltpu.make_async_copy(d, bd, in_sem.at[b, 1])]
        return [(jnp.logical_and(used, direct), copies(fused_cand.at[hh, l % 2], down_cand.at[hh, l % 2])),
                (jnp.logical_and(used, jnp.logical_not(direct)), copies(fused_hot.at[hh, l], down_hot.at[hh, l]))]

    def outputs(k):
        l, t = items[k]
        b = k % DEPTH
        put = [pltpu.make_async_copy(vf.at[b], fused_out.at[l, t], out_sem.at[b, 0]),
               pltpu.make_async_copy(vd.at[b], down_out.at[l, t], out_sem.at[b, 1])]
        if t < HOME:
            return [(None, put)]
        used = map_ref[flat, t - HOME] >= 0
        zero = [pltpu.make_async_copy(zf, fused_out.at[l, t], out_sem.at[b, 0]),
                pltpu.make_async_copy(zd, down_out.at[l, t], out_sem.at[b, 1])]
        return [(used, put), (jnp.logical_not(used), zero)]

    def run(groups, verb):
        for cond, copies in groups:
            def act():
                for c in copies:
                    getattr(c, verb)()
            if cond is None:
                act()
            else:
                pl.when(cond)(act)

    n = len(items)
    for k in range(n + LAG):
        if k < n:
            if k >= DEPTH:
                run(outputs(k - DEPTH)[:1] if items[k - DEPTH][1] < HOME else outputs(k - DEPTH), 'wait')
            run(inputs(k), 'start')
        if k >= LAG:
            run(inputs(k - LAG), 'wait')
            run(outputs(k - LAG), 'start')
    for k in range(n - DEPTH, n):
        run(outputs(k), 'wait')


def solution(mesh):
    flat_axes = ('stage', 'expert')
    S = jax.ShapeDtypeStruct
    cand = (S((HOT, LOCAL_LAYERS, HIDDEN, 2 * WIDTH), BF16), S((HOT, LOCAL_LAYERS, WIDTH, HIDDEN), BF16))
    home = (S((LAYERS, HOME, HIDDEN, 2 * WIDTH), BF16), S((LAYERS, HOME, WIDTH, HIDDEN), BF16))
    hot = (S((HOT, LAYERS, HIDDEN, 2 * WIDTH), BF16), S((HOT, LAYERS, WIDTH, HIDDEN), BF16))
    outs = (S((LAYERS, SLOTS, HIDDEN, 2 * WIDTH), BF16), S((LAYERS, SLOTS, WIDTH, HIDDEN), BF16))
    DMA = pltpu.SemaphoreType.DMA

    pick = pl.pallas_call(
        pick_kernel, out_shape=cand, in_specs=[SMEM, ANY, ANY, ANY], out_specs=(ANY, ANY),
        scratch_shapes=[pltpu.VMEM((LOCAL_LAYERS, HIDDEN, 2 * WIDTH), BF16), pltpu.VMEM((LOCAL_LAYERS, WIDTH, HIDDEN), BF16),
                        DMA((LOCAL_LAYERS, 5))])

    def exchange(owners):
        return pl.pallas_call(
            functools.partial(exchange_kernel, owners), out_shape=(*home, *hot), in_specs=[ANY] * 5, out_specs=(ANY,) * 4,
            scratch_shapes=[DMA((2, 2, 3)), DMA((4, 3)), DMA((HOT, 2, 3, 2)), DMA((HOT, 2, 3, 2)),
                            DMA((HOT, 2, 4, 2)), DMA((HOT, 2, 4, 2))],
            compiler_params=pltpu.CompilerParams(has_side_effects=True))

    place = pl.pallas_call(
        place_kernel, out_shape=outs, in_specs=[SMEM, SMEM] + [ANY] * 9, out_specs=(ANY, ANY),
        scratch_shapes=[pltpu.VMEM((DEPTH, HIDDEN, 2 * WIDTH), BF16), pltpu.VMEM((DEPTH, WIDTH, HIDDEN), BF16),
                        pltpu.VMEM((HIDDEN, 2 * WIDTH), BF16), pltpu.VMEM((WIDTH, HIDDEN), BF16),
                        DMA((DEPTH, 3)), DMA((DEPTH, 2)), DMA((2,))],
        compiler_params=pltpu.CompilerParams(vmem_limit_bytes=48 * 1024 * 1024))

    def local(gate, up, down, hot_units, slot_map):
        fused_cand, down_cand = pick(hot_units, gate, up, down)
        owner = hot_units // LOCAL_EXPERTS
        received = lax.switch(owner[0] * 2 + owner[1], [exchange((a, b)) for a in range(2) for b in range(2)],
                              gate, up, down, fused_cand, down_cand)
        return place(hot_units, slot_map, gate, up, down, fused_cand, down_cand, *received)

    return jax.shard_map(local, mesh=mesh, in_specs=(P('stage', 'expert'), P('stage', 'expert'), P('stage', 'expert'), P(), P()),
                         out_specs=(P(None, flat_axes), P(None, flat_axes)), check_vma=False)
```

time: 2840 us -> 834 us (0.29)
  waiting for transfers between devices: 1800 us -> 0 us
  Pallas kernels: 0 us -> 825 us
  local copies, waits for them, and re-layouts: 436 us -> 0.68 us
  starting transfers between devices: 396 us -> 0 us
  other arithmetic: 167 us -> 0.01 us
    psum x1 -> x0, waiting for transfers between devices: 1450 us -> none  [local_handover(): lax.psum(jnp.where(owned_mask, jnp.take(fused_home, local_pick, axis=1),...]
    pallas_call x0 -> x3, Pallas kernels: none -> 825 us  [the longest x1 764 us: local(): lax.switch(owner[0] * 2 + owner[1], [exchange((a, b)) for a in range(2) f...]
    ppermute x2 -> x0, starting transfers between devices: 379 us -> none  [the longest x1 252 us: local_handover(): fused_home = lax.ppermute(fused_recv, flat_axes, perm_pairs)]
    all_to_all x2 -> x0, waiting for transfers between devices: 350 us -> none  [the longest x1 350 us: local_handover(): lax.all_to_all(fused_send, 'stage', 1, 0, tiled=True)]
    another operation x122 -> x0, local copies, waits for them, and re-layouts: 272 us -> none  [the longest x49 114 us: local_handover(): jnp.take(fused_home, local_pick, axis=1)]
    concatenate x3 -> x0, other arithmetic: 90.3 us -> none  [the longest x1 44.7 us: local_handover(): jnp.concatenate([fused_home, fused_extra], axis=1)]
    select_n x4 -> x1, other arithmetic: 76.1 us -> 0.01 us  [local(): owner = hot_units // LOCAL_EXPERTS]
    gather x4 -> x0, local copies, waits for them, and re-layouts: 70.3 us -> none  [the longest x1 22.8 us: local_handover(): jnp.take(fused_home, local_pick, axis=1)]
  transfers between devices with their start and end apart: 5 -> 0, of which waited for: 2 -> 0; matrix products, arithmetic and copies ran while one was open for 3% -> 0% of each run, Pallas kernels for 0% -> 0%
where the time goes in v1:
time: 834 us; the launch traced here: 828 us
  Pallas kernels  825 us (99%)
    pallas_call x1, Pallas kernels, local(): lax.switch(owner[0] * 2 + owner[1], [exchange((a, b)) for a in range(2) f...  764 us
    pallas_call x1, Pallas kernels, local(): place(hot_units, slot_map, gate, up, down, fused_cand, down_cand, *received)  60.1 us

profile of v1, /device:TPU:0, one launch (start us, length us, event | category | flops | bytes accessed | tf_op | source)
XLA Modules:
  0.0 827.6 jit_solution(836377243820801515)
XLA Ops:
  0.6 0.0 copy-start
  0.6 0.9 shard_map.68
  1.6 0.0 copy-done
  1.6 0.6 fusion
  3.5 0.0 copy-start.1
  3.5 763.9 %conditional.1 = ((bf16[8,2,1024,1024]{3,2,1,0:T(8,128)(2,1)}, bf16[8,2,512,1024]{3,2,1,0:T(8,128)(2,1)}, bf16[2,8,1024,1024]{3,2,1,0:T(8,128)(2,1)}, bf16[2,8,512,1024]{3,2,1,0:T(8,128)(2,1)})) conditional(s32[]{:T(128)} %bitcast, (bf16[2,8,1024,512]{3,2,1,0:T(8,128)(2,1)}, bf16[2,8,1024,512]{3,2,1,0:T(8,128)(2,1)}, ...), branch_computations={%region_0.1_spmd, %region_1.2_spmd, %region_2.3_spmd, %region_3.4_... | conditional | bytes 8 | solution.py:283
  3.5 763.9 %branch_3_fun.1 = (bf16[8,2,1024,1024]{3,2,1,0:T(8,128)(2,1)}, bf16[8,2,512,1024]{3,2,1,0:T(8,128)(2,1)}, bf16[2,8,1024,1024]{3,2,1,0:T(8,128)(2,1)}, bf16[2,8,512,1024]{3,2,1,0:T(8,128)(2,1)}) custom-call(bf16[2,8,1024,512]{3,2,1,0:T(8,128)(2,1)} %get-tuple-element.55.gate, bf16[2,8,1024,512]{3,2,1,0:T(8,128)(2,1)} %get-tuple-element.56.up, ...), custom_call_target="tpu_custom_call" | custom-call | tf_op jit(solution)/shard_map/cond/branch_3_fun/pallas_call | solution.py:283
  767.4 0.0 copy-done.1
  767.5 0.1 copy.7.map_ref
  767.5 60.1 %shard_map.69 = (bf16[8,4,1024,1024]{3,2,1,0:T(8,128)(2,1)}, bf16[8,4,512,1024]{3,2,1,0:T(8,128)(2,1)}) custom-call(s32[2]{0:T(128)S(1)} %copy-done, s32[8,2]{1,0:T(8,128)S(1)} %copy.7.map_ref, bf16[2,8,1024,512]{3,2,1,0:T(8,128)(2,1)} %gate.3, bf16[2,8,1024,512]{3,2,1,0:T(8,128)(2,1)} %up.3, bf16[2,8,512,1024]{3,2,1,0:T(8,128)(2,1)} %down.3, ...), custom_call_target="tpu_custom_call" | custom-call | tf_op jit(solution)/shard_map/pallas_call | solution.py:285
  (1 shorter events, 0.0 us)
Async XLA Ops:
  0.6 1.0 copy-start
  3.5 763.9 %copy-start.1 = (s32[8,2]{0,1:T(2,128)S(1)}, s32[8,2]{0,1:T(2,128)}, u32[]{:S(2)}) copy-start(s32[8,2]{0,1:T(2,128)} %param.13) | copy-start | bytes 196

commit v2 on v1

v2 whole, which is shorter than its diff:
```python
import functools

import jax
import jax.numpy as jnp
from jax import lax
from jax.experimental import pallas as pl
from jax.experimental.pallas import tpu as pltpu
from jax.sharding import PartitionSpec as P

MESH = pl.DeviceIdType.MESH
ANY = pl.BlockSpec(memory_space=pl.ANY)
SMEM = pl.BlockSpec(memory_space=pltpu.SMEM)
BF16 = jnp.bfloat16
LAYERS, LOCAL_LAYERS, LOCAL_EXPERTS, HIDDEN, WIDTH = 8, 2, 8, 1024, 512
SLOTS, HOME, HOT = 4, 2, 2


def coords():
    stage, core = lax.axis_index('stage'), lax.axis_index('expert')
    return stage, core, stage // 2, stage % 2


def unit_reads(gate, up, down, a, e, dst, sem):
    return [pltpu.make_async_copy(gate.at[a, e], dst.at[pl.ds(0, HIDDEN), pl.ds(0, WIDTH)], sem.at[0]),
            pltpu.make_async_copy(up.at[a, e], dst.at[pl.ds(0, HIDDEN), pl.ds(WIDTH, WIDTH)], sem.at[1]),
            pltpu.make_async_copy(down.at[a, e], dst.at[pl.ds(HIDDEN, WIDTH)], sem.at[2])]


def pick_kernel(hot_ref, gate, up, down, cand, vm, sem):
    core = lax.axis_index('expert')
    for h in range(HOT):
        unit = hot_ref[h]

        @pl.when(unit // LOCAL_EXPERTS == core)
        def _():
            e = unit % LOCAL_EXPERTS
            ins = [unit_reads(gate, up, down, a, e, vm.at[h, a], sem.at[h, a]) for a in range(LOCAL_LAYERS)]
            outs = [pltpu.make_async_copy(vm.at[h, a], cand.at[h, a], sem.at[h, a, 3]) for a in range(LOCAL_LAYERS)]
            for group in ins:
                for c in group:
                    c.start()
            for group, out in zip(ins, outs):
                for c in group:
                    c.wait()
                out.start()
            for out in outs:
                out.wait()


def exchange_kernel(owners, gate, up, down, cand, fused_home, down_home, hot, late,
                    send_home, recv_home, send_hot, recv_hot, send_peer, recv_peer, vm, late_sem):
    stage, core, y, x = coords()
    ops = (gate, up, down)
    x_stage, y_stage, d_stage = y * 2 + (1 - x), (1 - y) * 2 + x, (1 - y) * 2 + (1 - x)
    xn, yn = (x_stage, core), (y_stage, core)

    def start(copies):
        for c in copies:
            c.start()

    def home_dsts(s, t0, count):
        rows, units = pl.ds(2 * s, 2), pl.ds(t0, count)
        return (fused_home.at[rows, units, :, pl.ds(0, WIDTH)], fused_home.at[rows, units, :, pl.ds(WIDTH, WIDTH)],
                down_home.at[rows, units])

    def home_copies(far, cc, t0):
        q = 1 - x if far else x
        dsts = home_dsts(stage, t0, 2 - t0)
        return [pltpu.make_async_remote_copy(
            src_ref=ops[k].at[:, pl.ds(q * 4 + cc * 2 + t0, 2 - t0)], dst_ref=dsts[k], send_sem=send_home.at[far, cc, k],
            recv_sem=recv_home.at[stage, k], device_id=(core * 2 + q, cc), device_id_type=MESH) for k in range(3)]

    def each_home(far, act):
        if far:
            act(home_copies(1, 1, 0))
            pl.when(core != y)(lambda: act(home_copies(1, 0, 0)))
            pl.when(core == y)(lambda: act(home_copies(1, 0, 1)))
        else:
            pl.when(core != y)(lambda: act(home_copies(0, 0, 0) + home_copies(0, 1, 1)))
            pl.when(jnp.logical_and(core == y, core == 0))(lambda: act(home_copies(0, 1, 0)))
            pl.when(jnp.logical_and(core == y, core == 1))(lambda: act(home_copies(0, 0, 0)))

    def remote(src, dst, ss, rs, device):
        return pltpu.make_async_remote_copy(src_ref=src, dst_ref=dst, send_sem=ss, recv_sem=rs, device_id=device,
                                            device_id_type=MESH)

    own_sends, forwards, peer = {}, {}, {}
    for h in range(HOT):
        for a in range(2):
            mine, dst = cand.at[h, a], hot.at[h, 2 * stage + a]
            own_sends[h, a] = (remote(mine, dst, send_hot.at[h, a, 0], recv_hot.at[h, a, 0], xn),
                               remote(mine, dst, send_hot.at[h, a, 1], recv_hot.at[h, a, 1], yn))
            piece = hot.at[h, 2 * (x_stage if a == 0 else y_stage) + a]
            forwards[h, a] = remote(piece, piece, send_hot.at[h, a, 2], recv_hot.at[h, a, 2], yn if a == 0 else xn)
            for r, origin in enumerate((stage, x_stage, y_stage, d_stage)):
                piece = hot.at[h, 2 * origin + a]
                peer[h, a, r] = remote(mine if r == 0 else piece, piece, send_peer.at[h, a, r], recv_peer.at[h, a, r],
                                       (stage, 1 - core))

    def arrival(h, a, r):
        piece = hot.at[h, 2 * (stage, x_stage, y_stage, d_stage)[r] + a]
        return remote(piece, piece, send_hot.at[h, a, r - 1], recv_hot.at[h, a, r - 1], xn)

    for h in range(HOT):
        @pl.when(core == owners[h])
        def _():
            for a in range(2):
                start(own_sends[h, a])
                peer[h, a, 0].start()

    each_home(0, start)
    each_home(1, start)

    late_unit = jnp.where(core == y, (1 - x) * 4, x * 4 + 2)
    reads = [unit_reads(gate, up, down, a, late_unit, vm.at[a], late_sem.at[a]) for a in range(2)]
    writes = [pltpu.make_async_copy(vm.at[a], late.at[a], late_sem.at[a, 3]) for a in range(2)]
    for group in reads:
        start(group)
    for group, write in zip(reads, writes):
        for c in group:
            c.wait()
        write.start()
    for write in writes:
        write.wait()

    for h in range(HOT):
        @pl.when(core == owners[h])
        def _():
            for a in range(2):
                arrival(h, a, a + 1).wait_recv()
                forwards[h, a].start()
                peer[h, a, a + 1].start()
            for a in range(2):
                arrival(h, a, 2 - a).wait_recv()
                peer[h, a, 2 - a].start()
    for h in range(HOT):
        @pl.when(core == owners[h])
        def _():
            for a in range(2):
                arrival(h, a, 3).wait_recv()
                peer[h, a, 3].start()

    for h in range(HOT):
        @pl.when(core == owners[h])
        def _():
            for a in range(2):
                for c in (*own_sends[h, a], forwards[h, a], *(peer[h, a, r] for r in range(4))):
                    c.wait_send()

        @pl.when(core != owners[h])
        def _():
            for a in range(2):
                for r in range(4):
                    peer[h, a, r].wait_recv()

    def sent(copies):
        for c in copies:
            c.wait_send()

    each_home(0, sent)
    each_home(1, sent)
    late_stage = jnp.where(core == 0, x_stage, y_stage)
    for s in range(4):
        def received(t0):
            for k, dst in enumerate(home_dsts(s, t0, 2 - t0)):
                remote(dst, dst, send_home.at[0, 0, k], recv_home.at[s, k], xn).wait_recv()

        pl.when(s == late_stage)(lambda: received(1))
        pl.when(jnp.logical_and(s != late_stage, jnp.logical_or(s != stage, core != y)))(lambda: received(0))


DEPTH, LAG = 10, 5


def place_kernel(hot_ref, map_ref, gate, up, down, cand, fused_home, down_home, hot,
                 fused_out, down_out, vm, zero, in_sem, out_sem):
    stage, core, y, x = coords()
    flat = stage * 2 + core
    late_stage = jnp.where(core == 0, y * 2 + (1 - x), (1 - y) * 2 + x)
    zero[...] = jnp.zeros_like(zero)
    items = [(l, t) for t in range(SLOTS) for l in range(LAYERS)]

    def inputs(k):
        l, t = items[k]
        b = k % DEPTH
        bf, bd = vm.at[b, pl.ds(0, HIDDEN)], vm.at[b, pl.ds(HIDDEN, WIDTH)]
        own = stage == l // 2
        if t < HOME:
            e = x * 4 + core * 2 + t
            direct = jnp.logical_and(own, core == y)
            arrived = [pltpu.make_async_copy(fused_home.at[l, t], bf, in_sem.at[b, 0]),
                       pltpu.make_async_copy(down_home.at[l, t], bd, in_sem.at[b, 1])]
            other = jnp.logical_not(direct)
            if t == 0:
                other = jnp.logical_and(other, late_stage != l // 2)
            return [(direct, unit_reads(gate, up, down, l % 2, e, vm.at[b], in_sem.at[b])), (other, arrived)]
        h = map_ref[flat, t - HOME]
        used = h >= 0
        hh = jnp.maximum(h, 0)
        direct = jnp.logical_and(own, hot_ref[hh] // LOCAL_EXPERTS == core)
        return [(jnp.logical_and(used, direct), [pltpu.make_async_copy(cand.at[hh, l % 2], vm.at[b], in_sem.at[b, 0])]),
                (jnp.logical_and(used, jnp.logical_not(direct)), [pltpu.make_async_copy(hot.at[hh, l], vm.at[b], in_sem.at[b, 0])])]

    def outputs(k):
        l, t = items[k]
        b = k % DEPTH

        def put(src):
            return [pltpu.make_async_copy(src.at[pl.ds(0, HIDDEN)], fused_out.at[l, t], out_sem.at[b, 0]),
                    pltpu.make_async_copy(src.at[pl.ds(HIDDEN, WIDTH)], down_out.at[l, t], out_sem.at[b, 1])]
        if t == 0:
            return [(late_stage != l // 2, put(vm.at[b]))]
        if t < HOME:
            return [(None, put(vm.at[b]))]
        used = map_ref[flat, t - HOME] >= 0
        return [(used, put(vm.at[b])), (jnp.logical_not(used), put(zero))]

    def run(groups, verb):
        for cond, copies in groups:
            def act():
                for c in copies:
                    getattr(c, verb)()
            if cond is None:
                act()
            else:
                pl.when(cond)(act)

    n = len(items)
    for k in range(n + LAG):
        if k < n:
            if k >= DEPTH:
                run(outputs(k - DEPTH), 'wait')
            run(inputs(k), 'start')
        if k >= LAG:
            run(inputs(k - LAG), 'wait')
            run(outputs(k - LAG), 'start')
    for k in range(n - DEPTH, n):
        run(outputs(k), 'wait')


def finish_kernel(late, fused_in, down_in, fused_out, down_out, vm, sem):
    del fused_in, down_in
    stage, core, y, x = coords()
    late_stage = jnp.where(core == 0, y * 2 + (1 - x), (1 - y) * 2 + x)
    reads = [pltpu.make_async_copy(late.at[a], vm.at[a], sem.at[a, 0]) for a in range(2)]
    for c in reads:
        c.start()
    writes = []
    for a in range(2):
        reads[a].wait()
        l = 2 * late_stage + a
        for c in (pltpu.make_async_copy(vm.at[a, pl.ds(0, HIDDEN)], fused_out.at[l, 0], sem.at[a, 1]),
                  pltpu.make_async_copy(vm.at[a, pl.ds(HIDDEN, WIDTH)], down_out.at[l, 0], sem.at[a, 2])):
            c.start()
            writes.append(c)
    for c in writes:
        c.wait()


def solution(mesh):
    flat_axes = ('stage', 'expert')
    S = jax.ShapeDtypeStruct
    ROWS = HIDDEN + WIDTH
    home = (S((LAYERS, HOME, HIDDEN, 2 * WIDTH), BF16), S((LAYERS, HOME, WIDTH, HIDDEN), BF16))
    outs = (S((LAYERS, SLOTS, HIDDEN, 2 * WIDTH), BF16), S((LAYERS, SLOTS, WIDTH, HIDDEN), BF16))
    DMA = pltpu.SemaphoreType.DMA

    pick = pl.pallas_call(
        pick_kernel, out_shape=S((HOT, LOCAL_LAYERS, ROWS, HIDDEN), BF16), in_specs=[SMEM, ANY, ANY, ANY], out_specs=ANY,
        scratch_shapes=[pltpu.VMEM((HOT, LOCAL_LAYERS, ROWS, HIDDEN), BF16), DMA((HOT, LOCAL_LAYERS, 4))])

    def exchange(owners):
        return pl.pallas_call(
            functools.partial(exchange_kernel, owners),
            out_shape=(*home, S((HOT, LAYERS, ROWS, HIDDEN), BF16), S((LOCAL_LAYERS, ROWS, HIDDEN), BF16)),
            in_specs=[ANY] * 4, out_specs=(ANY,) * 4,
            scratch_shapes=[DMA((2, 2, 3)), DMA((4, 3)), DMA((HOT, 2, 3)), DMA((HOT, 2, 3)), DMA((HOT, 2, 4)), DMA((HOT, 2, 4)),
                            pltpu.VMEM((LOCAL_LAYERS, ROWS, HIDDEN), BF16), DMA((LOCAL_LAYERS, 4))],
            compiler_params=pltpu.CompilerParams(has_side_effects=True))

    place = pl.pallas_call(
        place_kernel, out_shape=outs, in_specs=[SMEM, SMEM] + [ANY] * 7, out_specs=(ANY, ANY),
        scratch_shapes=[pltpu.VMEM((DEPTH, ROWS, HIDDEN), BF16), pltpu.VMEM((ROWS, HIDDEN), BF16), DMA((DEPTH, 3)), DMA((DEPTH, 2))],
        cost_estimate=pl.CostEstimate(flops=10 ** 9, bytes_accessed=2 * 10 ** 8, transcendentals=0),
        compiler_params=pltpu.CompilerParams(vmem_limit_bytes=48 * 1024 * 1024))

    finish = pl.pallas_call(
        finish_kernel, out_shape=outs, in_specs=[ANY] * 3, out_specs=(ANY, ANY), input_output_aliases={1: 0, 2: 1},
        scratch_shapes=[pltpu.VMEM((LOCAL_LAYERS, ROWS, HIDDEN), BF16), DMA((LOCAL_LAYERS, 3))])

    pairs = []
    for y in range(2):
        for x in range(2):
            pairs.append(((y * 2 + x) * 2 + y, (y * 2 + 1 - x) * 2))
            pairs.append(((y * 2 + x) * 2 + 1 - y, ((1 - y) * 2 + x) * 2 + 1))

    def local(gate, up, down, hot_units, slot_map):
        cand = pick(hot_units, gate, up, down)
        owner = hot_units // LOCAL_EXPERTS
        fused_home, down_home, hot, late = lax.switch(
            owner[0] * 2 + owner[1], [exchange((a, b)) for a in range(2) for b in range(2)], gate, up, down, cand)
        late = lax.ppermute(late, flat_axes, pairs)
        fused, down_out = place(hot_units, slot_map, gate, up, down, cand, fused_home, down_home, hot)
        return finish(late, fused, down_out)

    return jax.shard_map(local, mesh=mesh, in_specs=(P('stage', 'expert'), P('stage', 'expert'), P('stage', 'expert'), P(), P()),
                         out_specs=(P(None, flat_axes), P(None, flat_axes)), check_vma=False)
```

time: 834 us -> 779 us (0.934)
  Pallas kernels: 825 us -> 768 us
    pallas_call x1, Pallas kernels: 764 us -> 699 us  [local(): lax.switch(owner[0] * 2 + owner[1], [exchange((a, b)) for a in range(2) f...]
    pallas_call x2 -> x3, Pallas kernels: 61 us -> 68.2 us  [the longest x1 62.7 us: local(): place(hot_units, slot_map, gate, up, down, cand, fused_home, down_home, hot)]
  transfers between devices with their start and end apart: 0 -> 1, of which waited for: 0 -> 1; matrix products, arithmetic and copies ran while one was open for 0% -> 0% of each run, Pallas kernels for 0% -> 8%
where the time goes in v2:
time: 779 us
  Pallas kernels  768 us (99%)
    pallas_call x1, Pallas kernels, local(): lax.switch(owner[0] * 2 + owner[1], [exchange((a, b)) for a in range(2) f...  699 us
    pallas_call x1, Pallas kernels, local(): place(hot_units, slot_map, gate, up, down, cand, fused_home, down_home, hot)  62.7 us
  transfers between devices with their start and end apart: 1, of which 1 were waited for; matrix products, arithmetic and copies ran while one was open for 0% of the time, Pallas kernels for 8%

profile of v2, /device:TPU:0, one launch (start us, length us, event | category | flops | bytes accessed | tf_op | source)
XLA Modules:
  0.0 779.1 jit_solution(11428794179570181940)
XLA Ops:
  0.6 0.7 and_select_fusion
  1.3 0.6 fusion
  1.9 0.9 shard_map.68.cand
  4.0 0.0 copy-start.1
  4.1 0.0 copy-start
  4.1 699.4 %conditional.1 = ((bf16[8,2,1024,1024]{3,2,1,0:T(8,128)(2,1)}, bf16[8,2,512,1024]{3,2,1,0:T(8,128)(2,1)}, bf16[2,8,1536,1024]{3,2,1,0:T(8,128)(2,1)}, bf16[2,1536,1024]{2,1,0:T(8,128)(2,1)})) conditional(s32[]{:T(128)} %bitcast, (bf16[2,8,1024,512]{3,2,1,0:T(8,128)(2,1)}, bf16[2,8,1024,512]{3,2,1,0:T(8,128)(2,1)}, ...), branch_computations={%region_0.1_spmd, %region_1.2_spmd, %region_2.3_spmd, %region_3.4_... | conditional | bytes 8 | solution.py:300
  4.1 699.4 %branch_3_fun.1 = (bf16[8,2,1024,1024]{3,2,1,0:T(8,128)(2,1)}, bf16[8,2,512,1024]{3,2,1,0:T(8,128)(2,1)}, bf16[2,8,1536,1024]{3,2,1,0:T(8,128)(2,1)}, bf16[2,1536,1024]{2,1,0:T(8,128)(2,1)}) custom-call(bf16[2,8,1024,512]{3,2,1,0:T(8,128)(2,1)} %get-tuple-element.44.gate, bf16[2,8,1024,512]{3,2,1,0:T(8,128)(2,1)} %get-tuple-element.45.up, ...), custom_call_target="tpu_custom_call" | custom-call | tf_op jit(solution)/shard_map/cond/branch_3_fun/pallas_call | solution.py:300
  703.5 1.5 collective-permute-start
  705.0 0.0 copy-done.1
  705.0 0.1 copy.9.map_ref
  705.0 0.0 copy-done
  705.0 62.7 %shard_map.69 = (bf16[8,4,1024,1024]{3,2,1,0:T(8,128)(2,1)}, bf16[8,4,512,1024]{3,2,1,0:T(8,128)(2,1)}) custom-call(s32[2]{0:T(128)S(1)} %copy-done, s32[8,2]{1,0:T(8,128)S(1)} %copy.9.map_ref, bf16[2,8,1024,512]{3,2,1,0:T(8,128)(2,1)} %gate.3, bf16[2,8,1024,512]{3,2,1,0:T(8,128)(2,1)} %up.3, bf16[2,8,512,1024]{3,2,1,0:T(8,128)(2,1)} %down.3, ...), custom_call_target="tpu_custom_call" | custom-call | flops 1000000000 | bytes 200000000 | tf_op jit(solution)/shard_map/pallas_call | solution.py:303
  767.7 6.8 collective-permute-done.late
  774.5 4.6 shard_map.70
Async XLA Ops:
  4.0 700.9 %copy-start.1 = (s32[8,2]{0,1:T(2,128)S(1)}, s32[8,2]{0,1:T(2,128)}, u32[]{:S(2)}) copy-start(s32[8,2]{0,1:T(2,128)} %param.13) | copy-start | bytes 196
  4.1 701.0 %copy-start = (s32[2]{0:T(128)S(1)}, s32[2]{0:T(128)}, u32[]{:S(2)}) copy-start(s32[2]{0:T(128)} %hot_ref.3) | copy-start | bytes 28
  703.5 71.0 %collective-permute-start = (bf16[2,1536,1024]{2,1,0:T(8,128)(2,1)}, bf16[2,1536,1024]{2,1,0:T(8,128)(2,1)}, u32[]{:S(2)}, u32[]{:S(2)}) collective-permute-start(bf16[2,1536,1024]{2,1,0:T(8,128)(2,1)} %get-tuple-element.56), channel_id=1, source_target_pairs={{0,2},{1,5},{2,0},{3,7},{5,6},{4,1},{7,4},{6,3}} | collective-permute-start | bytes 18874376 | tf_op jit(solution)/shard_map/ppermute | solution.py:302
